TPU v7x, 256 devices: a whole 4x4x8 slice. The times are simulated.
256 devices in a mesh: rep: 8 (over x_lo, y), tp: 8 (over z), fs: 4 (over x_hi, core).
Axes of the slice: x: 4 (x_hi: 2, x_lo: 2; x = x_hi * 2 + x_lo), y: 4, z: 8, core: 2. Of those that a mesh axis runs over, the one named last changes fastest.
Arguments:
- hidden: bfloat16 [64, 8192], P(('rep', 'fs'), 'tp'), may hold values from -6 to 6
- cache_key: bfloat16 [64, 2048, 1024], P(('rep', 'fs'), None, 'tp'), may hold values from -1300 to 1300
- cache_value: bfloat16 [64, 2048, 1024], P(('rep', 'fs'), None, 'tp'), may hold values from -6 to 6
- lengths: int32 [64], P(('rep', 'fs')), may hold values from 8 to 2047
- owner: int32 [1], replicated, may hold values from 0 to 32767
- query_weight: bfloat16 [8, 8192, 4096], P('rep', 'fs', 'tp'), may hold values from -0.0625 to 0.0625
- key_weight: bfloat16 [8, 8192, 1024], P('rep', 'fs', 'tp'), may hold values from -0.0625 to 0.0625
- value_weight: bfloat16 [8, 8192, 1024], P('rep', 'fs', 'tp'), may hold values from -0.0625 to 0.0625
- out_weight: bfloat16 [8, 4096, 8192], P('rep', 'tp', 'fs'), may hold values from -0.09375 to 0.09375
Outputs:
- mixed: bfloat16 [64, 8192], P(('rep', 'fs'), 'tp')
- new_key: bfloat16 [64, 1024], P(('rep', 'fs'), 'tp')
- new_value: bfloat16 [64, 1024], P(('rep', 'fs'), 'tp')
- fresh_query: bfloat16 [8, 8192, 4096], P('rep', 'fs', 'tp')
- fresh_key: bfloat16 [8, 8192, 1024], P('rep', 'fs', 'tp')
- fresh_value: bfloat16 [8, 8192, 1024], P('rep', 'fs', 'tp')
- fresh_out: bfloat16 [8, 4096, 8192], P('rep', 'tp', 'fs')
Inputs may be any that keep to these rules, and one draw needn't show every extreme that they name: `lengths`: the number of positions already in each sequence's cache; the new token stands at that position.
All inputs are finite; a program needn't handle non-finite values.
Results may differ from a plain program's by a relative error of at most 0.0065.
Values may be sent and summed in bfloat16 or wider, within the bound.
No kernel may reach another device: no remote copies, remote signals or barrier semaphores. Data moves between devices by JAX's collectives and lax.ppermute only.
A program may use at most 64 MiB of HBM per device.

v0:
```python
import jax
import jax.numpy as jnp
from jax import lax
from jax.sharding import PartitionSpec as P

DH = 128


rope_base = 500000.0
epsilon = 1e-05


def from_root(shard, axis, root):
    mine = lax.axis_index(axis) == root
    return lax.psum(jnp.where(mine, shard, jnp.zeros_like(shard)), axis)


def cut_along(shard, dim, peers):
    lengths = shard.shape
    parts = shard.reshape(*lengths[:dim], peers, lengths[dim] // peers, *lengths[dim + 1 :])
    return jnp.moveaxis(parts, dim, 0)


def sent_and_summed(shard, axis, dim):
    peers = lax.axis_size(axis)
    parts = lax.all_to_all(cut_along(shard, dim, peers), axis, 0, 0, tiled=True)
    return jnp.sum(parts, axis=0)


def copy_for_each(shard, axis):
    peers = lax.axis_size(axis)
    return lax.all_to_all(
        jnp.broadcast_to(shard[None], (peers, *shard.shape)), axis, 0, 0, tiled=True
    )


def joined_along(parts, dim):
    parts = jnp.moveaxis(parts, 0, dim)
    lengths = parts.shape
    return parts.reshape(*lengths[:dim], lengths[dim] * lengths[dim + 1], *lengths[dim + 2 :])


def collect(shard, axis, dim):
    parts = copy_for_each(shard, axis)
    return joined_along(parts, dim)


def rotate(heads, positions):
    half_dim = heads.shape[-1] // 2
    frequency = rope_base ** (-(jnp.arange(half_dim, dtype=jnp.float32) * 2.0 / heads.shape[-1]))
    angles = positions.astype(jnp.float32)[:, None] * frequency[None, :]
    cosine = jnp.cos(angles)[:, None, :]
    sine_part = jnp.sin(angles)[:, None, :]
    first_half = heads[..., :half_dim]
    second_half = heads[..., half_dim:]
    return jnp.concatenate(
        [
            first_half * cosine - second_half * sine_part,
            second_half * cosine + first_half * sine_part,
        ],
        axis=-1,
    )


def attend(query, own_key, own_value, cache_key, cache_value, lengths):
    seqs, span, width = cache_key.shape
    kv_local = query.shape[1]
    head_size = query.shape[3]
    keys_view = cache_key.reshape(seqs, span, kv_local, head_size)
    values_view = cache_value.reshape(seqs, span, kv_local, head_size)
    scale = head_size ** (-0.5)
    scores = (
        jnp.einsum("shgd,sthd->shgt", query, keys_view, preferred_element_type=jnp.float32) * scale
    )
    own_score = (
        jnp.einsum("shgd,shd->shg", query, own_key, preferred_element_type=jnp.float32) * scale
    )
    live = (jnp.arange(span, dtype=jnp.int32)[None, :] < lengths[:, None])[:, None, None, :]
    masked = jnp.where(live, scores, -jnp.inf)
    row_max = jnp.maximum(jnp.max(masked, axis=-1), own_score)
    weights = jnp.where(live, jnp.exp(scores - row_max[..., None]), 0.0)
    own_weight = jnp.exp(own_score - row_max)
    denominator = jnp.sum(weights, axis=-1) + own_weight
    probs = (weights / denominator[..., None]).astype(jnp.bfloat16)
    own_prob = (own_weight / denominator).astype(jnp.bfloat16)
    context = jnp.einsum("shgt,sthd->shgd", probs, values_view, preferred_element_type=jnp.float32)
    return (
        context
        + own_prob.astype(jnp.float32)[..., None] * own_value.astype(jnp.float32)[:, :, None, :]
    )


def local(
    hidden,
    cache_key,
    cache_value,
    lengths,
    owner,
    query_weight,
    key_weight,
    value_weight,
    out_weight,
):
    owner_rank = owner[0] % lax.axis_size("rep")
    features = lax.all_gather(hidden, "tp", axis=1, tiled=True)
    hidden_wide = features.astype(jnp.float32)
    normed = (
        hidden_wide
        * lax.rsqrt(jnp.mean(hidden_wide * hidden_wide, axis=-1, keepdims=True) + epsilon)
    ).astype(jnp.bfloat16)
    fresh_query, fresh_key, fresh_value, fresh_out = (
        from_root(query_weight, "rep", owner_rank),
        from_root(key_weight, "rep", owner_rank),
        from_root(value_weight, "rep", owner_rank),
        from_root(out_weight, "rep", owner_rank),
    )
    query_rows = fresh_query[0]
    key_rows = fresh_key[0]
    value_rows = fresh_value[0]
    out_cols = fresh_out[0]
    seqs = normed.shape[0]
    query_width = query_rows.shape[1]
    key_width = key_rows.shape[1]
    token_block = lax.all_to_all(normed, "fs", split_axis=1, concat_axis=0, tiled=True)
    joined = sent_and_summed(
        jnp.concatenate(
            [
                jnp.dot(token_block, query_rows, preferred_element_type=jnp.float32),
                jnp.dot(token_block, key_rows, preferred_element_type=jnp.float32),
                jnp.dot(token_block, value_rows, preferred_element_type=jnp.float32),
            ],
            axis=1,
        ),
        "fs",
        0,
    )
    query_proj = joined[:, :query_width]
    key_proj = joined[:, query_width : query_width + key_width]
    value_proj = joined[:, query_width + key_width :]
    q_heads = query_proj.shape[1] // DH
    kv_heads = key_proj.shape[1] // DH
    query_rot = rotate(query_proj.reshape(seqs, q_heads, DH), lengths).astype(jnp.bfloat16)
    query_rot = query_rot.reshape(seqs, kv_heads, q_heads // kv_heads, DH)
    key_new = rotate(key_proj.reshape(seqs, kv_heads, DH), lengths).astype(jnp.bfloat16)
    value_new = value_proj.astype(jnp.bfloat16).reshape(seqs, kv_heads, DH)
    context = attend(query_rot, key_new, value_new, cache_key, cache_value, lengths)
    context = context.astype(jnp.bfloat16).reshape(seqs, q_heads * DH)
    group_context = collect(context, "fs", 0)
    partial_out = jnp.dot(group_context, out_cols, preferred_element_type=jnp.float32)
    terms = lax.all_to_all(partial_out, "fs", split_axis=0, concat_axis=1, tiled=True)
    summed = sent_and_summed(terms, "tp", 1)
    mixed = (summed + hidden.astype(jnp.float32)).astype(jnp.bfloat16)
    return (
        mixed,
        key_new.reshape(seqs, kv_heads * DH),
        value_new.reshape(seqs, kv_heads * DH),
        fresh_query,
        fresh_key,
        fresh_value,
        fresh_out,
    )


def solution(mesh):
    return jax.shard_map(
        local,
        mesh=mesh,
        in_specs=(
            P(("rep", "fs"), "tp"),
            P(("rep", "fs"), None, "tp"),
            P(("rep", "fs"), None, "tp"),
            P(("rep", "fs")),
            P(),
            P("rep", "fs", "tp"),
            P("rep", "fs", "tp"),
            P("rep", "fs", "tp"),
            P("rep", "tp", "fs"),
        ),
        out_specs=(
            P(("rep", "fs"), "tp"),
            P(("rep", "fs"), "tp"),
            P(("rep", "fs"), "tp"),
            P("rep", "fs", "tp"),
            P("rep", "fs", "tp"),
            P("rep", "fs", "tp"),
            P("rep", "tp", "fs"),
        ),
        check_vma=False,
    )
```

profile of v0, /device:TPU:1, one launch (start us, length us, event | category | flops | bytes accessed | tf_op | source)
XLA Modules:
  0.0 207.0 jit_solution(11398649867773513769)
XLA Ops:
  7.2 0.0 copy-start
  7.2 0.0 all-reduce.3.cloned.1.call-start
  8.0 0.0 copy-start.2
  8.0 3.2 %broadcast_select_fusion = bf16[1,512,2048]{2,1,0:T(8,128)(2,1)} fusion(bf16[1,512,2048]{2,1,0:T(8,128)(2,1)} %param.17, pred[]{:T(512)S(6)} %eq.4), kind=kLoop, calls=%fused_computation.5 | loop fusion | flops 1048576 | bytes 4194305 | tf_op jit(solution)/shard_map/jit(_where)/select_n | solution.py:15
  11.2 0.0 copy-done.2
  11.2 0.0 copy-start.7
  11.2 0.0 copy-start.8
  11.2 1.5 broadcast_select_fusion.1
  12.7 0.0 copy-done.7
  12.7 0.1 copy-done.8
  12.8 1.0 broadcast_select_fusion.2
  13.8 0.0 copy-start.9
  13.8 0.0 copy-start.10
  13.8 0.0 all-reduce.3.cloned.1.call-update
  13.8 0.7 copy-done.9
  14.5 23.9 %all_gather.3 = bf16[2,8192]{1,0:T(2,128)(2,1)S(1)} all-gather(bf16[2,1024]{1,0:T(2,128)(2,1)S(1)} %copy-done.9), channel_id=1, replica_groups=mesh['rep'=8,'tp'=8,'fs'=4] {'tp'}, dimensions={1}, use_global_device_ids=true | all-gather | bytes 36864 | tf_op jit(solution)/shard_map/all_gather | solution.py:105
  38.4 0.2 fusion.10
  38.6 0.7 fusion.11
  39.3 10.1 %all-to-all-start = ((bf16[2,4,2048]{2,0,1:T(2,128)(2,1)}), bf16[2,4,2048]{2,0,1:T(2,128)(2,1)S(1)}, u32[]{:S(2)}, u32[]{:S(2)}) async-start(bf16[2,4,2048]{2,0,1:T(2,128)(2,1)} %bitcast), calls=%async_computation | async-start | bytes 65536 | tf_op jit(solution)/shard_map/all_to_all | solution.py:124
  49.4 0.0 copy-done.10
  49.4 0.1 iota_compare_fusion
  49.6 5.2 %all-to-all-done = bf16[2,4,2048]{2,0,1:T(2,128)(2,1)S(1)} async-done(((bf16[2,4,2048]{2,0,1:T(2,128)(2,1)}), bf16[2,4,2048]{2,0,1:T(2,128)(2,1)S(1)}, u32[]{:S(2)}, u32[]{:S(2)}) %all-to-all-start) | async-done | bytes 32800 | tf_op jit(solution)/shard_map/all_to_all | solution.py:124
  54.7 92.3 %all-reduce.3.cloned.1.call-done = (bf16[1,2048,128]{2,1,0:T(8,128)(2,1)}, bf16[1,2048,128]{2,1,0:T(8,128)(2,1)}, bf16[1,2048,512]{2,1,0:T(8,128)(2,1)}, bf16[1,512,2048]{2,1,0:T(8,128)(2,1)}) async-done(((bf16[1,2048,128]{2,1,0:T(8,128)(2,1)}, bf16[1,2048,128]{2,1,0:T(8,128)(2,1)}, bf16[1,2048,512]{2,1,0:T(8,128)(2,1)}, bf16[1,512,2048]{2,1,0:T(8,128)(2,1)}), (bf16[1,2048,128]{2,1,0:T(8,128)(2,1)}, ...) | async-done | bytes 5242896 | tf_op jit(solution)/shard_map/psum | solution.py:15
  147.0 0.0 copy-start.5
  147.0 0.0 copy-start.3
  147.0 2.0 fusion.2
  149.1 0.0 copy-start.1
  149.1 0.0 copy-done.5
  149.1 0.2 fusion.8
  149.3 0.0 copy-done.3
  149.3 0.2 fusion.6
  149.5 0.6 reshape.245
  150.1 4.8 %all-to-all-start.1 = ((f32[4,2,768]{2,1,0:T(2,128)}), f32[4,2,768]{2,1,0:T(2,128)S(1)}, u32[]{:S(2)}, u32[]{:S(2)}) async-start(f32[4,2,768]{2,1,0:T(2,128)} %reshape.245), calls=%async_computation.1 | async-start | bytes 49152 | tf_op jit(solution)/shard_map/all_to_all | solution.py:26
  154.9 0.1 multiply_cosine_fusion.1
  155.0 4.5 %all-to-all-done.1 = f32[4,2,768]{2,1,0:T(2,128)S(1)} async-done(((f32[4,2,768]{2,1,0:T(2,128)}), f32[4,2,768]{2,1,0:T(2,128)S(1)}, u32[]{:S(2)}, u32[]{:S(2)}) %all-to-all-start.1) | async-done | bytes 24608 | tf_op jit(solution)/shard_map/all_to_all | solution.py:26
  159.6 0.5 fusion.32
  160.1 0.1 fusion.28
  160.2 0.1 fusion.39
  160.3 0.1 subtract_convert_fusion
  160.4 0.2 fusion.25
  160.6 0.0 copy-done
  160.6 0.5 select_reduce_fusion
  161.1 0.2 fusion.12
  161.3 1.5 fusion.5
  162.9 7.7 %all_to_all.47 = bf16[4,2,512]{2,1,0:T(2,128)(2,1)S(1)} all-to-all(bf16[4,2,512]{2,1,0:T(2,128)(2,1)S(1)} %broadcast_in_dim.52), channel_id=1, replica_groups=mesh['rep'=8,'tp'=8,'fs'=4] {'fs'}, dimensions={0} | all-to-all | bytes 16384 | tf_op jit(solution)/shard_map/all_to_all | solution.py:32
  170.6 0.0 copy-done.1
  170.6 0.4 fusion
  171.0 8.5 %all_to_all.48 = f32[4,2,2048]{2,1,0:T(2,128)} all-to-all(f32[4,2,2048]{2,1,0:T(2,128)S(1)} %fusion), channel_id=1, replica_groups=mesh['rep'=8,'tp'=8,'fs'=4] {'fs'}, dimensions={0} | all-to-all | bytes 131072 | tf_op jit(solution)/shard_map/all_to_all | solution.py:150
  179.5 6.7 %all-to-all-start.4 = ((f32[8,2,1024]{2,1,0:T(2,128)}), f32[8,2,1024]{2,1,0:T(2,128)S(1)}, u32[]{:S(2)}, u32[]{:S(2)}) async-start(f32[8,2,1024]{2,1,0:T(2,128)} %bitcast.16), calls=%async_computation.4 | async-start | bytes 131072 | tf_op jit(solution)/shard_map/all_to_all | solution.py:26
  186.2 0.6 pad_maximum_fusion.2
  186.8 6.6 %all-to-all-done.4 = f32[8,2,1024]{2,1,0:T(2,128)S(1)} async-done(((f32[8,2,1024]{2,1,0:T(2,128)}), f32[8,2,1024]{2,1,0:T(2,128)S(1)}, u32[]{:S(2)}, u32[]{:S(2)}) %all-to-all-start.4) | async-done | bytes 65568 | tf_op jit(solution)/shard_map/all_to_all | solution.py:26
  193.5 0.6 add_convert_fusion
  194.1 0.0 copy-start.6
  194.1 0.0 copy-start.4
  194.1 3.1 %copy.34 = bf16[1,2048,512]{2,1,0:T(8,128)(2,1)} copy(bf16[1,2048,512]{2,1,0:T(8,128)(2,1)} %get-tuple-element.28) | data formatting | bytes 4194304
  197.2 0.0 copy-done.6
  197.2 0.8 copy.35
  198.0 0.0 copy-done.4
  198.0 0.8 copy.36
  198.8 1.3 copy.37
  (14 shorter events, 0.2 us)
Async XLA Ops:
  7.2 153.4 %copy-start = (bf16[2,2048,128]{2,1,0:T(8,128)(2,1)S(1)}, bf16[2,2048,128]{2,1,0:T(8,128)(2,1)}, u32[]{:S(2)}) copy-start(bf16[2,2048,128]{2,1,0:T(8,128)(2,1)} %param.10) | copy-start | bytes 3145732
  7.2 139.8 %all-reduce.3.cloned.1.call-start = ((), (), s32[]{:S(2)}) async-start(), calls=%async_computation.5 | async-start | bytes 10485760 | tf_op jit(solution)/shard_map/psum | solution.py:15
  8.0 3.2 %copy-start.2 = (bf16[1,2048,512]{2,1,0:T(8,128)(2,1)S(1)}, bf16[1,2048,512]{2,1,0:T(8,128)(2,1)}, u32[]{:S(2)}) copy-start(bf16[1,2048,512]{2,1,0:T(8,128)(2,1)} %param.14) | copy-start | bytes 6291460
  11.2 1.5 copy-start.7
  11.2 1.6 copy-start.8
  13.8 0.7 copy-start.9
  13.8 35.6 %copy-start.10 = (s32[2]{0:T(128)S(1)}, s32[2]{0:T(128)}, u32[]{:S(2)}) copy-start(s32[2]{0:T(128)} %param.12) | copy-start | bytes 28
  39.3 15.4 %all-to-all-start = ((bf16[2,4,2048]{2,0,1:T(2,128)(2,1)}), bf16[2,4,2048]{2,0,1:T(2,128)(2,1)S(1)}, u32[]{:S(2)}, u32[]{:S(2)}) async-start(bf16[2,4,2048]{2,0,1:T(2,128)(2,1)} %bitcast), calls=%async_computation | async-start | bytes 65536 | tf_op jit(solution)/shard_map/all_to_all | solution.py:124
  147.0 2.1 copy-start.5
  147.0 2.2 %copy-start.3 = (bf16[1,2048,128]{2,1,0:T(8,128)(2,1)S(1)}, bf16[1,2048,128]{2,1,0:T(8,128)(2,1)}, u32[]{:S(2)}) copy-start(bf16[1,2048,128]{2,1,0:T(8,128)(2,1)} %get-tuple-element.30) | copy-start | bytes 1572868
  149.1 21.5 %copy-start.1 = (bf16[1,512,2048]{2,1,0:T(8,128)(2,1)S(1)}, bf16[1,512,2048]{2,1,0:T(8,128)(2,1)}, u32[]{:S(2)}) copy-start(bf16[1,512,2048]{2,1,0:T(8,128)(2,1)} %get-tuple-element.31) | copy-start | bytes 6291460
  150.1 9.4 %all-to-all-start.1 = ((f32[4,2,768]{2,1,0:T(2,128)}), f32[4,2,768]{2,1,0:T(2,128)S(1)}, u32[]{:S(2)}, u32[]{:S(2)}) async-start(f32[4,2,768]{2,1,0:T(2,128)} %reshape.245), calls=%async_computation.1 | async-start | bytes 49152 | tf_op jit(solution)/shard_map/all_to_all | solution.py:26
  179.5 14.0 %all-to-all-start.4 = ((f32[8,2,1024]{2,1,0:T(2,128)}), f32[8,2,1024]{2,1,0:T(2,128)S(1)}, u32[]{:S(2)}, u32[]{:S(2)}) async-start(f32[8,2,1024]{2,1,0:T(2,128)} %bitcast.16), calls=%async_computation.4 | async-start | bytes 131072 | tf_op jit(solution)/shard_map/all_to_all | solution.py:26
  194.1 3.1 %copy-start.6 = (bf16[1,2048,128]{2,1,0:T(8,128)(2,1)S(1)}, bf16[1,2048,128]{2,1,0:T(8,128)(2,1)}, u32[]{:S(2)}) copy-start(bf16[1,2048,128]{2,1,0:T(8,128)(2,1)} %get-tuple-element.29) | copy-start | bytes 1572868
  194.1 3.9 %copy-start.4 = (bf16[1,2048,128]{2,1,0:T(8,128)(2,1)S(1)}, bf16[1,2048,128]{2,1,0:T(8,128)(2,1)}, u32[]{:S(2)}) copy-start(bf16[1,2048,128]{2,1,0:T(8,128)(2,1)} %get-tuple-element.30) | copy-start | bytes 1572868
Sparse Core Ops, SparseCore 0:
  14.0 133.0 all-reduce.2
where the time goes:
time: 208 us; the launch traced here: 207 us
  waiting for transfers between devices  109 us (52%)
  blocking collectives  40.1 us (19%)
  starting transfers between devices  21.7 us (10%)
  between operations  14.9 us (7%)
  other arithmetic  9.02 us (4%)
  local copies, waits for them, and re-layouts  7.55 us (4%)
  matrix products  5.08 us (2%)
    psum x1, waiting for transfers between devices, from_root(): return lax.psum(jnp.where(mine, shard, jnp.zeros_like(shard)), axis)  92.3 us
    all_gather x1, blocking collectives, local(): features = lax.all_gather(hidden, 'tp', axis=1, tiled=True)  23.9 us
    all_to_all x2, starting transfers between devices, sent_and_summed(): parts = lax.all_to_all(cut_along(shard, dim, peers), axis, 0, 0, tiled=True)  11.5 us
    all_to_all x2, waiting for transfers between devices, sent_and_summed(): parts = lax.all_to_all(cut_along(shard, dim, peers), axis, 0, 0, tiled=True)  11.2 us
    all_to_all x1, starting transfers between devices, local(): lax.all_to_all(normed, 'fs', split_axis=1, concat_axis=0, tiled=True)  10.1 us
    all_to_all x1, blocking collectives, local(): lax.all_to_all(partial_out, 'fs', split_axis=0, concat_axis=1, tiled=True)  8.51 us
    all_to_all x1, blocking collectives, copy_for_each(): lax.all_to_all(jnp.broadcast_to(shard[None], (peers, *shard.shape)), axis...  7.7 us
    unnamed x27, local copies, waits for them, and re-layouts  6.86 us
  transfers between devices with their start and end apart: 4, of which 4 were waited for; matrix products, arithmetic and copies ran while one was open for 1% of the time, Pallas kernels for 0%

commit v1 on v0

--- a/solution.py
+++ b/solution.py
@@ -90,6 +90,12 @@
     )
 
 
+def from_owner(parts, owner_rank):
+    peers = lax.axis_size("rep")
+    grouped = parts.reshape(peers, parts.shape[0] // peers, *parts.shape[1:])
+    return lax.dynamic_index_in_dim(grouped, owner_rank, 0, keepdims=False)
+
+
 def local(
     hidden,
     cache_key,
@@ -101,39 +107,38 @@
     value_weight,
     out_weight,
 ):
-    owner_rank = owner[0] % lax.axis_size("rep")
-    features = lax.all_gather(hidden, "tp", axis=1, tiled=True)
-    hidden_wide = features.astype(jnp.float32)
-    normed = (
-        hidden_wide
-        * lax.rsqrt(jnp.mean(hidden_wide * hidden_wide, axis=-1, keepdims=True) + epsilon)
-    ).astype(jnp.bfloat16)
+    reps, fss, tps = lax.axis_size("rep"), lax.axis_size("fs"), lax.axis_size("tp")
+    owner_rank = owner[0] % reps
     fresh_query, fresh_key, fresh_value, fresh_out = (
         from_root(query_weight, "rep", owner_rank),
         from_root(key_weight, "rep", owner_rank),
         from_root(value_weight, "rep", owner_rank),
         from_root(out_weight, "rep", owner_rank),
     )
-    query_rows = fresh_query[0]
-    key_rows = fresh_key[0]
-    value_rows = fresh_value[0]
-    out_cols = fresh_out[0]
-    seqs = normed.shape[0]
-    query_width = query_rows.shape[1]
-    key_width = key_rows.shape[1]
-    token_block = lax.all_to_all(normed, "fs", split_axis=1, concat_axis=0, tiled=True)
-    joined = sent_and_summed(
-        jnp.concatenate(
-            [
-                jnp.dot(token_block, query_rows, preferred_element_type=jnp.float32),
-                jnp.dot(token_block, key_rows, preferred_element_type=jnp.float32),
-                jnp.dot(token_block, value_rows, preferred_element_type=jnp.float32),
-            ],
-            axis=1,
-        ),
-        "fs",
-        0,
+    seqs = hidden.shape[0]
+    hidden_wide = collect(hidden, "tp", 1).astype(jnp.float32)
+    normed = (
+        hidden_wide
+        * lax.rsqrt(jnp.mean(hidden_wide * hidden_wide, axis=-1, keepdims=True) + epsilon)
+    ).astype(jnp.bfloat16)
+    blocks = cut_along(normed, 1, fss)
+    blocks = jnp.broadcast_to(blocks[None], (reps, *blocks.shape))
+    blocks = blocks.reshape(reps * fss, *blocks.shape[2:])
+    tokens = lax.all_to_all(blocks, ("rep", "fs"), 0, 0, tiled=True)
+    tokens = tokens.reshape(reps * fss * seqs, tokens.shape[-1])
+    query_width = query_weight.shape[2]
+    key_width = key_weight.shape[2]
+    partial = jnp.concatenate(
+        [
+            jnp.dot(tokens, query_weight[0], preferred_element_type=jnp.float32),
+            jnp.dot(tokens, key_weight[0], preferred_element_type=jnp.float32),
+            jnp.dot(tokens, value_weight[0], preferred_element_type=jnp.float32),
+        ],
+        axis=1,
     )
+    partial = partial.reshape(reps * fss, seqs, partial.shape[1])
+    shares = lax.all_to_all(partial, ("rep", "fs"), 0, 0, tiled=True)
+    joined = jnp.sum(from_owner(shares, owner_rank), axis=0)
     query_proj = joined[:, :query_width]
     key_proj = joined[:, query_width : query_width + key_width]
     value_proj = joined[:, query_width + key_width :]
@@ -145,9 +150,13 @@
     value_new = value_proj.astype(jnp.bfloat16).reshape(seqs, kv_heads, DH)
     context = attend(query_rot, key_new, value_new, cache_key, cache_value, lengths)
     context = context.astype(jnp.bfloat16).reshape(seqs, q_heads * DH)
-    group_context = collect(context, "fs", 0)
-    partial_out = jnp.dot(group_context, out_cols, preferred_element_type=jnp.float32)
-    terms = lax.all_to_all(partial_out, "fs", split_axis=0, concat_axis=1, tiled=True)
+    contexts = lax.all_to_all(
+        jnp.broadcast_to(context[None], (reps * fss, *context.shape)), ("rep", "fs"), 0, 0, tiled=True
+    ).reshape(reps * fss * seqs, q_heads * DH)
+    partial_out = jnp.dot(contexts, out_weight[0], preferred_element_type=jnp.float32)
+    partial_out = partial_out.reshape(reps * fss, seqs, partial_out.shape[1])
+    terms = lax.all_to_all(partial_out, ("rep", "fs"), 0, 0, tiled=True)
+    terms = joined_along(from_owner(terms, owner_rank), 1)
     summed = sent_and_summed(terms, "tp", 1)
     mixed = (summed + hidden.astype(jnp.float32)).astype(jnp.bfloat16)
     return (

time: 208 us -> 178 us (0.86)
  waiting for transfers between devices: 109 us -> 43.2 us
  blocking collectives: 40.1 us -> 71.5 us
  local copies, waits for them, and re-layouts: 7.55 us -> 11.8 us
  other arithmetic: 9.02 us -> 6.06 us
    psum x1, waiting for transfers between devices: 92.3 us -> 23.6 us  [from_root(): return lax.psum(jnp.where(mine, shard, jnp.zeros_like(shard)), axis)]
    all_to_all x2 -> x3, blocking collectives: 16.2 us -> 71.5 us  [the longest x1 40.5 us: local(): lax.all_to_all(jnp.broadcast_to(context[None], (reps * fss, *context.shap...]
    all_gather x1 -> x0, blocking collectives: 23.9 us -> none  [local(): features = lax.all_gather(hidden, 'tp', axis=1, tiled=True)]
    all_to_all x3, waiting for transfers between devices: 16.4 us -> 19.6 us  [the longest x1 9.43 us: local(): shares = lax.all_to_all(partial, ('rep', 'fs'), 0, 0, tiled=True)]
  transfers between devices with their start and end apart: 4 -> 4, of which waited for: 4 -> 4; matrix products, arithmetic and copies ran while one was open for 1% -> 9% of each run, Pallas kernels for 0% -> 0%
where the time goes in v1:
time: 178 us; the launch traced here: 177 us
  blocking collectives  71.5 us (40%)
  waiting for transfers between devices  43.2 us (24%)
  starting transfers between devices  23.7 us (13%)
  between operations  14.9 us (8%)
  local copies, waits for them, and re-layouts  11.8 us (7%)
  other arithmetic  6.06 us (3%)
  matrix products  5.73 us (3%)
    all_to_all x1, blocking collectives, local(): lax.all_to_all(jnp.broadcast_to(context[None], (reps * fss, *context.shap...  40.5 us
    psum x1, waiting for transfers between devices, from_root(): return lax.psum(jnp.where(mine, shard, jnp.zeros_like(shard)), axis)  23.6 us
    all_to_all x1, blocking collectives, local(): terms = lax.all_to_all(partial_out, ('rep', 'fs'), 0, 0, tiled=True)  18.9 us
    all_to_all x1, blocking collectives, sent_and_summed(): parts = lax.all_to_all(cut_along(shard, dim, peers), axis, 0, 0, tiled=True)  12.1 us
    all_to_all x1, waiting for transfers between devices, local(): shares = lax.all_to_all(partial, ('rep', 'fs'), 0, 0, tiled=True)  9.43 us
    all_to_all x1, starting transfers between devices, local(): tokens = lax.all_to_all(blocks, ('rep', 'fs'), 0, 0, tiled=True)  9.25 us
    all_to_all x1, waiting for transfers between devices, local(): tokens = lax.all_to_all(blocks, ('rep', 'fs'), 0, 0, tiled=True)  9.01 us
    all_to_all x1, starting transfers between devices, copy_for_each(): lax.all_to_all(jnp.broadcast_to(shard[None], (peers, *shard.shape)), axis...  9 us
  transfers between devices with their start and end apart: 4, of which 4 were waited for; matrix products, arithmetic and copies ran while one was open for 9% of the time, Pallas kernels for 0%

profile of v1, /device:TPU:1, one launch (start us, length us, event | category | flops | bytes accessed | tf_op | source)
XLA Modules:
  0.0 176.9 jit_solution(9229973164668991891)
XLA Ops:
  7.2 0.0 copy-start
  7.2 1.4 broadcast_in_dim.31
  8.6 9.0 %all-to-all-start = ((bf16[8,2,1024]{2,1,0:T(2,128)(2,1)}), bf16[8,2,1024]{2,1,0:T(2,128)(2,1)S(1)}, u32[]{:S(2)}, u32[]{:S(2)}) async-start(bf16[8,2,1024]{2,1,0:T(2,128)(2,1)} %broadcast_in_dim.31), calls=%async_computation | async-start | bytes 65536 | tf_op jit(solution)/shard_map/all_to_all | solution.py:32
  17.6 0.0 all-reduce.3.cloned.1.call-start
  18.3 0.0 copy-start.1
  18.3 1.5 broadcast_select_fusion
  19.8 0.9 copy-done.1
  20.6 0.0 copy-start.3
  20.6 0.0 copy-start.4
  20.6 1.5 broadcast_select_fusion.1
  22.1 0.0 copy-done.3
  22.1 0.1 copy-done.4
  22.2 1.0 broadcast_select_fusion.2
  23.3 0.0 copy-start.9
  23.3 0.0 all-reduce.3.cloned.1.call-update
  23.3 1.2 all-to-all-done
  24.6 0.2 fusion.10
  24.7 0.1 fusion.13
  24.9 0.9 broadcast_in_dim.32
  25.8 9.2 %all-to-all-start.1 = ((bf16[32,2,2048]{2,1,0:T(2,128)(2,1)}), bf16[32,2,2048]{2,1,0:T(2,128)(2,1)}, u32[]{:S(2)}, u32[]{:S(2)}) async-start(bf16[32,2,2048]{2,1,0:T(2,128)(2,1)} %bitcast.2), calls=%async_computation.1 | async-start | bytes 524288 | tf_op jit(solution)/shard_map/all_to_all | solution.py:127
  35.0 0.0 copy-done.9
  35.0 0.1 iota_compare_fusion
  35.2 9.0 %all-to-all-done.1 = bf16[32,2,2048]{2,1,0:T(2,128)(2,1)} async-done(((bf16[32,2,2048]{2,1,0:T(2,128)(2,1)}), bf16[32,2,2048]{2,1,0:T(2,128)(2,1)}, u32[]{:S(2)}, u32[]{:S(2)}) %all-to-all-start.1) | async-done | bytes 262176 | tf_op jit(solution)/shard_map/all_to_all | solution.py:127
  44.2 1.0 reshape.261
  45.2 1.3 fusion.6
  46.5 1.3 fusion.8
  47.8 0.5 fusion.2
  48.2 0.0 copy-start.2
  48.3 0.8 reshape.262
  49.1 5.5 %all-to-all-start.2 = ((f32[32,2,768]{2,1,0:T(2,128)}), f32[32,2,768]{2,1,0:T(2,128)S(1)}, u32[]{:S(2)}, u32[]{:S(2)}) async-start(f32[32,2,768]{2,1,0:T(2,128)} %reshape.262), calls=%async_computation.2 | async-start | bytes 393216 | tf_op jit(solution)/shard_map/all_to_all | solution.py:140
  54.5 0.1 multiply_cosine_fusion.1
  54.7 9.4 %all-to-all-done.2 = f32[32,2,768]{2,1,0:T(2,128)S(1)} async-done(((f32[32,2,768]{2,1,0:T(2,128)}), f32[32,2,768]{2,1,0:T(2,128)S(1)}, u32[]{:S(2)}, u32[]{:S(2)}) %all-to-all-start.2) | async-done | bytes 196640 | tf_op jit(solution)/shard_map/all_to_all | solution.py:140
  64.1 0.1 fusion.29
  64.2 0.5 fusion.33
  64.8 0.0 copy-start.10
  64.8 0.1 subtract_convert_fusion
  64.9 0.2 fusion.26
  65.0 0.0 copy-done
  65.0 0.5 select_reduce_fusion
  65.6 0.2 fusion.12
  65.8 1.5 fusion.5
  67.3 0.1 broadcast_in_dim.36
  67.4 40.5 %all_to_all.30 = bf16[32,2,512]{2,1,0:T(2,128)(2,1)S(1)} all-to-all(bf16[32,2,512]{2,1,0:T(2,128)(2,1)S(1)} %broadcast_in_dim.36), channel_id=1, replica_groups=mesh['rep'=8,'tp'=8,'fs'=4] {'rep','fs'}, dimensions={0} | all-to-all | bytes 131072 | tf_op jit(solution)/shard_map/all_to_all | solution.py:153
  107.9 0.0 copy-done.2
  107.9 0.0 copy-start.8
  107.9 0.5 fusion
  108.4 0.0 copy-done.10
  108.4 0.4 copy.21
  108.8 18.9 %all_to_all.31 = f32[32,2,2048]{2,1,0:T(2,128)S(1)} all-to-all(f32[32,2,2048]{2,1,0:T(2,128)S(1)} %copy.21), channel_id=1, replica_groups=mesh['rep'=8,'tp'=8,'fs'=4] {'rep','fs'}, dimensions={0} | all-to-all | bytes 1048576 | tf_op jit(solution)/shard_map/all_to_all | solution.py:158
  127.7 12.1 %all_to_all.32 = f32[8,2,1024]{2,1,0:T(2,128)S(1)} all-to-all(f32[8,2,1024]{2,1,0:T(2,128)S(1)} %bitcast.51), channel_id=1, replica_groups=mesh['rep'=8,'tp'=8,'fs'=4] {'tp'}, dimensions={0} | all-to-all | bytes 131072 | tf_op jit(solution)/shard_map/all_to_all | solution.py:26
  139.8 0.0 copy-done.8
  139.8 0.6 add_convert_fusion
  140.4 23.6 %all-reduce.3.cloned.1.call-done = (bf16[1,2048,512]{2,1,0:T(8,128)(2,1)}, bf16[1,2048,128]{2,1,0:T(8,128)(2,1)}, bf16[1,2048,128]{2,1,0:T(8,128)(2,1)}, bf16[1,512,2048]{2,1,0:T(8,128)(2,1)}) async-done(((bf16[1,2048,512]{2,1,0:T(8,128)(2,1)}, bf16[1,2048,128]{2,1,0:T(8,128)(2,1)}, bf16[1,2048,128]{2,1,0:T(8,128)(2,1)}, bf16[1,512,2048]{2,1,0:T(8,128)(2,1)}), (bf16[1,2048,512]{2,1,0:T(8,128)(2,1)}, ...) | async-done | bytes 5242896 | tf_op jit(solution)/shard_map/psum | solution.py:15
  164.0 0.0 copy-start.7
  164.0 0.0 copy-start.6
  164.0 0.0 copy-start.5
  164.0 3.2 %copy.36 = bf16[1,2048,512]{2,1,0:T(8,128)(2,1)} copy(bf16[1,2048,512]{2,1,0:T(8,128)(2,1)} %get-tuple-element.29) | data formatting | bytes 4194304
  167.2 0.0 copy-done.7
  167.2 0.8 copy.37
  168.0 0.0 copy-done.6
  168.0 0.8 copy.38
  168.8 0.0 copy-done.5
  168.8 1.3 copy.39
  (17 shorter events, 0.3 us)
Async XLA Ops:
  7.2 57.9 %copy-start = (bf16[2,2048,128]{2,1,0:T(8,128)(2,1)S(1)}, bf16[2,2048,128]{2,1,0:T(8,128)(2,1)}, u32[]{:S(2)}) copy-start(bf16[2,2048,128]{2,1,0:T(8,128)(2,1)} %param.10) | copy-start | bytes 3145732
  8.6 15.9 %all-to-all-start = ((bf16[8,2,1024]{2,1,0:T(2,128)(2,1)}), bf16[8,2,1024]{2,1,0:T(2,128)(2,1)S(1)}, u32[]{:S(2)}, u32[]{:S(2)}) async-start(bf16[8,2,1024]{2,1,0:T(2,128)(2,1)} %broadcast_in_dim.31), calls=%async_computation | async-start | bytes 65536 | tf_op jit(solution)/shard_map/all_to_all | solution.py:32
  17.6 146.4 %all-reduce.3.cloned.1.call-start = ((), (), s32[]{:S(2)}) async-start(), calls=%async_computation.6 | async-start | bytes 10485760 | tf_op jit(solution)/shard_map/psum | solution.py:15
  18.3 2.4 %copy-start.1 = (bf16[1,2048,512]{2,1,0:T(8,128)(2,1)S(1)}, bf16[1,2048,512]{2,1,0:T(8,128)(2,1)}, u32[]{:S(2)}) copy-start(bf16[1,2048,512]{2,1,0:T(8,128)(2,1)} %param.14) | copy-start | bytes 6291460
  20.6 1.5 copy-start.3
  20.6 1.6 copy-start.4
  23.3 11.8 %copy-start.9 = (s32[2]{0:T(128)S(1)}, s32[2]{0:T(128)}, u32[]{:S(2)}) copy-start(s32[2]{0:T(128)} %param.12) | copy-start | bytes 28
  25.8 18.4 %all-to-all-start.1 = ((bf16[32,2,2048]{2,1,0:T(2,128)(2,1)}), bf16[32,2,2048]{2,1,0:T(2,128)(2,1)}, u32[]{:S(2)}, u32[]{:S(2)}) async-start(bf16[32,2,2048]{2,1,0:T(2,128)(2,1)} %bitcast.2), calls=%async_computation.1 | async-start | bytes 524288 | tf_op jit(solution)/shard_map/all_to_all | solution.py:127
  48.2 59.6 %copy-start.2 = (bf16[1,512,2048]{2,1,0:T(8,128)(2,1)S(1)}, bf16[1,512,2048]{2,1,0:T(8,128)(2,1)}, u32[]{:S(2)}) copy-start(bf16[1,512,2048]{2,1,0:T(8,128)(2,1)} %param.17) | copy-start | bytes 6291460
  49.1 15.0 %all-to-all-start.2 = ((f32[32,2,768]{2,1,0:T(2,128)}), f32[32,2,768]{2,1,0:T(2,128)S(1)}, u32[]{:S(2)}, u32[]{:S(2)}) async-start(f32[32,2,768]{2,1,0:T(2,128)} %reshape.262), calls=%async_computation.2 | async-start | bytes 393216 | tf_op jit(solution)/shard_map/all_to_all | solution.py:140
  64.8 43.6 %copy-start.10 = (bf16[2,128]{1,0:T(2,128)(2,1)}, bf16[2,128]{1,0:T(2,128)(2,1)S(1)}, u32[]{:S(2)}) copy-start(bf16[2,128]{1,0:T(2,128)(2,1)S(1)} %get-tuple-element.27) | copy-start | bytes 1540
  107.9 31.9 %copy-start.8 = (bf16[2,1024]{1,0:T(2,128)(2,1)S(1)}, bf16[2,1024]{1,0:T(2,128)(2,1)}, u32[]{:S(2)}) copy-start(bf16[2,1024]{1,0:T(2,128)(2,1)} %param.9) | copy-start | bytes 12292
  164.0 3.2 %copy-start.7 = (bf16[1,2048,128]{2,1,0:T(8,128)(2,1)S(1)}, bf16[1,2048,128]{2,1,0:T(8,128)(2,1)}, u32[]{:S(2)}) copy-start(bf16[1,2048,128]{2,1,0:T(8,128)(2,1)} %get-tuple-element.30) | copy-start | bytes 1572868
  164.0 4.0 %copy-start.6 = (bf16[1,2048,128]{2,1,0:T(8,128)(2,1)S(1)}, bf16[1,2048,128]{2,1,0:T(8,128)(2,1)}, u32[]{:S(2)}) copy-start(bf16[1,2048,128]{2,1,0:T(8,128)(2,1)} %get-tuple-element.31) | copy-start | bytes 1572868
  164.0 4.8 %copy-start.5 = (bf16[1,512,2048]{2,1,0:T(8,128)(2,1)S(1)}, bf16[1,512,2048]{2,1,0:T(8,128)(2,1)}, u32[]{:S(2)}) copy-start(bf16[1,512,2048]{2,1,0:T(8,128)(2,1)} %get-tuple-element.32) | copy-start | bytes 6291460
Sparse Core Ops, SparseCore 0:
  23.4 140.5 all-reduce.2
